TPU v7x, 256 devices: a whole 4x4x8 slice. The times are simulated.
256 devices in a mesh: wa: 64 (over x_hi, y, z), ba: 4 (over x_lo, core).
Axes of the slice: x: 4 (x_hi: 2, x_lo: 2; x = x_hi * 2 + x_lo), y: 4, z: 8, core: 2. Of those that a mesh axis runs over, the one named last changes fastest.
Arguments:
- latent: float32 [16, 8, 8192], P('ba', None, 'wa'), parts along dimension 0, may hold values from -12 to 12
- noise: float32 [2, 16, 8, 8192], P(None, 'ba', None, 'wa'), parts along dimension 1, may hold values from -6 to 6
- offsets: int32 [128], P('wa'), may hold values from 0 to 63
- anchors: int32 [2], replicated, may hold values from 0 to 127
- guidance: float32 [1], replicated, may hold values from 0.4 to 0.8
- w_in: bfloat16 [320, 36], replicated, may hold values from -1 to 1
- w_mid: bfloat16 [320, 320], replicated, may hold values from -0.3125 to 0.3125
- w_out: bfloat16 [36, 320], replicated, may hold values from -0.109375 to 0.109375
- t_embed: float32 [2, 320], replicated, may hold values from -6 to 6
- w_feat: float32 [64, 4], replicated, may hold values from -3 to 3
Outputs:
- denoised: float32 [16, 8, 8192], P('ba', None, 'wa'), parts along dimension 0
There are 4 independent parts, one for each index of `ba`. A program takes and returns all parts, laid end to end along the dimension named above; an argument that names none is the same for every part. Nothing has to cross between parts.
All inputs are finite; a program needn't handle non-finite values.
Results may differ from a plain program's by a relative error of at most 0.0065.
Values sent between devices are 32-bit elements; how exact they have to be, the bound alone decides.
No kernel may reach another device: no remote copies, remote signals or barrier semaphores. Data moves between devices by JAX's collectives and lax.ppermute only.
A program may use at most 64 MiB of HBM per device.

v0:
```python
import math
import jax
import jax.numpy as jnp
from jax import lax
from jax.sharding import Mesh
from jax.sharding import PartitionSpec as P

WIN = 128
STRIDE = 64
STEPS = 2
WA = ("wa_0", "wa_1", "wa_2")
TAP_SHIFTS = ((-1, -1), (-1, 0), (-1, 1), (0, -1), (0, 0), (0, 1), (1, -1), (1, 0), (1, 1))
CUMULATIVE_ALPHA = (0.35, 0.55, 0.72, 0.85, 0.93)
STABILITY = 1e-06


def broadcast_by_axis(shard, axes, root):
    shard = jnp.where(lax.axis_index(axes) == root, shard, jnp.zeros_like(shard))
    for axis in axes:
        shard = lax.psum(shard, axis)
    return shard


def from_everyone(shard, axis):
    copies = jnp.broadcast_to(shard, (lax.axis_size(axis), *shard.shape))
    return lax.all_to_all(copies, axis, split_axis=0, concat_axis=0, tiled=True)


def of_everyone(shard, axis):
    return from_everyone(shard, axis).sum(axis=0)


def passed_along(shard, axis, by):
    length = lax.axis_size(axis)
    return lax.ppermute(shard, axis, [(i, (i + by) % length) for i in range(length)])


def plan(number):
    current = CUMULATIVE_ALPHA[number]
    following = CUMULATIVE_ALPHA[number + 1]
    spread = 0.3 * math.sqrt(1.0 - following)
    return (
        math.sqrt(current),
        math.sqrt(1.0 - current),
        math.sqrt(following),
        math.sqrt(1.0 - following - spread * spread),
        spread,
    )


def tapped(field):
    height, columns = (field.shape[-2], field.shape[-1])
    padding = [(0, 0)] * (field.ndim - 2) + [(1, 1), (1, 1)]
    padded = jnp.pad(field, padding)
    return jnp.stack(
        [
            padded[..., 1 + down_by : 1 + down_by + height, 1 + right_by : 1 + right_by + columns]
            for down_by, right_by in TAP_SHIFTS
        ]
    )


def denoise(window, w_in, w_mid, w_out, embedding):
    channels, height, columns = window.shape
    stacked = tapped(window.astype(jnp.bfloat16)).reshape(9 * channels, height * columns)
    hidden_in = jnp.dot(w_in, stacked, preferred_element_type=jnp.float32) + embedding[:, None]
    activated = jax.nn.silu(hidden_in).astype(jnp.bfloat16)
    middle = jnp.dot(w_mid, activated, preferred_element_type=jnp.float32)
    joined = (hidden_in + jax.nn.silu(middle)).astype(jnp.bfloat16)
    outward = jnp.dot(w_out, joined, preferred_element_type=jnp.float32).reshape(
        9, channels, height, columns
    )
    padded = jnp.pad(outward, ((0, 0), (0, 0), (1, 1), (1, 1)))
    result = jnp.zeros((channels, height, columns), jnp.float32)
    for index, (down_by, right_by) in enumerate(TAP_SHIFTS):
        result = (
            result
            + padded[
                index, :, 1 + down_by : 1 + down_by + height, 1 + right_by : 1 + right_by + columns
            ]
        )
    return result


def clean_of(windows, w_in, w_mid, w_out, embedding, now_a, now_s):
    predicted = jax.vmap(denoise, (0, None, None, None, None))(
        windows, w_in, w_mid, w_out, embedding
    )
    cleaned = (windows - now_s * predicted) / now_a
    return (cleaned, predicted)


def percept(cleaned, w_feat):
    return jax.nn.silu(jnp.einsum("fc,chw->fhw", w_feat, cleaned, precision=lax.Precision.HIGHEST))


def mismatch(cleaned, anchor_percept, w_feat):
    difference = percept(cleaned, w_feat) - anchor_percept
    return 0.5 * jnp.sum(difference * difference) / w_feat.shape[0]


def finish_gradient(cleaned, pullback, anchor_percept, w_feat):
    clean_grad = jax.vmap(jax.grad(mismatch), (0, None, None))(cleaned, anchor_percept, w_feat)
    return pullback(clean_grad)[0]


def advance(windows, gradient, predicted, scale, now_a, now_s, next_a, direction):
    return next_a * (windows - scale * gradient - now_s * predicted) / now_a + direction * predicted


def window_update(extended, number, starts, anchors, guidance, w_in, w_mid, w_out, t_embed, w_feat):
    per_dev = starts.shape[0]
    now_a, now_s, next_a, direction, spread = plan(number)
    embedding = t_embed[number]
    windows = jnp.stack(
        [lax.dynamic_slice_in_dim(extended, starts[index], WIN, 2) for index in range(per_dev)]
    )

    def cleaning(inputs):
        return clean_of(inputs, w_in, w_mid, w_out, embedding, now_a, now_s)

    cleaned, pullback, predicted = jax.vjp(cleaning, windows, has_aux=True)
    owner = anchors[number] // per_dev
    slot = anchors[number] % per_dev
    picked = lax.dynamic_index_in_dim(cleaned, slot, 0, keepdims=False)
    anchor_percept = percept(broadcast_by_axis(picked, WA, owner), w_feat)
    gradient = finish_gradient(cleaned, pullback, anchor_percept, w_feat)
    square_sum = of_everyone(jnp.sum(gradient * gradient), WA)
    element_count = per_dev * lax.axis_size(WA) * windows.shape[1] * windows.shape[2] * WIN
    scale = guidance[0] * lax.rsqrt(square_sum / element_count + STABILITY)
    advanced = advance(windows, gradient, predicted, scale, now_a, now_s, next_a, direction)
    summed = jnp.zeros(extended.shape, jnp.float32)
    for index in range(per_dev):
        current = lax.dynamic_slice_in_dim(summed, starts[index], WIN, 2)
        summed = lax.dynamic_update_slice_in_dim(
            summed, current + advanced[index], starts[index], 2
        )
    return (summed, spread)


def local(latent, noise, offsets, anchors, guidance, w_in, w_mid, w_out, t_embed, w_feat):
    width = latent.shape[-1]
    per_dev = offsets.shape[0]
    starts = jnp.arange(per_dev, dtype=jnp.int32) * STRIDE + offsets
    positions = jnp.arange(2 * width, dtype=jnp.int32)
    inside = (positions[None, :] >= starts[:, None]) & (positions[None, :] < starts[:, None] + WIN)
    cover = jnp.sum(inside.astype(jnp.float32), axis=0)
    count_own = cover[:width] + passed_along(cover[width:], WA, 1)
    state = latent
    for number in range(STEPS):
        neighbour = passed_along(state, WA, -1)
        extended = jnp.concatenate([state, neighbour], axis=2)
        summed, spread = window_update(
            extended, number, starts, anchors, guidance, w_in, w_mid, w_out, t_embed, w_feat
        )
        spill = passed_along(summed[:, :, width:], WA, 1)
        state = (summed[:, :, :width] + spill) / count_own + spread * noise[number]
    return state


def solution(mesh):
    finer = Mesh(mesh.devices.reshape(2, 4, 8, mesh.shape["ba"]), ("wa_0", "wa_1", "wa_2", "ba"))
    placed = (P("ba", None, WA), P(None, "ba", None, WA), P(WA), P(), P(), P(), P(), P(), P(), P())
    return jax.shard_map(
        local, mesh=finer, in_specs=placed, out_specs=P("ba", None, WA), check_vma=False
    )
```

profile of v0, /device:TPU:2, one launch (start us, length us, event | category | flops | bytes accessed | tf_op | source)
XLA Modules:
  0.0 238.8 jit_solution(6218011149825673397)
XLA Ops:
  0.0 0.8 fusion.239
  0.8 9.9 %collective-permute-start = (f32[4,8,128]{2,0,1:T(4,128)S(1)}, f32[4,8,128]{2,0,1:T(4,128)S(1)}, u32[]{:S(2)}, u32[]{:S(2)}) collective-permute-start(f32[4,8,128]{2,0,1:T(4,128)S(1)} %get-tuple-element.43), channel_id=1, source_target_pairs={{0,252},{4,0},{8,4},{12,8},{16,12},{20,16},{24,20},{28,24},{32,28}... | collective-permute-start | bytes 49160 | tf_op jit(solution)/shard_map/ppermute | solution.py:35
  10.6 0.7 broadcast_add_fusion
  11.4 0.6 slice.200
  12.0 0.6 fusion.241
  12.6 1.4 slice_reduce_fusion
  13.9 1.4 fusion.240
  22.7 0.1 reshape.151
  22.8 1.3 fusion.190
  24.1 2.6 %fusion.88 = f32[2,1024,320]{1,2,0:T(8,128)} fusion(f32[2,1024,320]{1,2,0:T(8,128)S(1)} %fusion.190, f32[320]{0:T(512)S(1)} %get-tuple-element.6, bf16[320,320]{1,0:T(8,128)(2,1)S(1)} %copy-done), kind=kOutput, calls=%fused_computation.107 | convolution fusion | flops 423362560 | bytes 5448960 | tf_op jit(solution)/shard_map/jvp(vmap())/dot_general | solution.py:68
  26.7 2.6 %fusion.94 = f32[2,36,1024]{2,1,0:T(8,128)S(1)} fusion(f32[2,1024,320]{1,2,0:T(8,128)} %fusion.88, f32[2,1024,320]{1,2,0:T(8,128)S(1)} %fusion.190, f32[320]{0:T(512)S(1)} %get-tuple-element.6, bf16[36,320]{1,0:T(8,128)(2,1)S(1)} %copy-done.3), kind=kOutput, calls=%fused_computation.112 | convolution fusion | flops 51773440 | bytes 5562112 | tf_op jit(solution)/shard_map/jvp(vmap())/dot_general | solution.py:70
  29.5 0.2 fusion.180
  29.7 9.6 %psum.42 = f32[4,8,128]{2,0,1:T(4,128)S(1)} all-reduce(f32[4,8,128]{2,0,1:T(4,128)S(1)} %select_bitcast_fusion.1), channel_id=1, replica_groups=mesh['wa_0'=2,'wa_1'=4,'wa_2'=8,'ba'=4] {'wa_0'}, use_global_device_ids=true, to_apply=%region_0.0 | all-reduce | flops 4096 | bytes 32768 | tf_op jit(solution)/shard_map/psum | solution.py:20
  39.2 14.3 %psum.43 = f32[4,8,128]{2,0,1:T(4,128)S(1)} all-reduce(f32[4,8,128]{2,0,1:T(4,128)S(1)} %psum.42), channel_id=1, replica_groups=mesh['wa_0'=2,'wa_1'=4,'wa_2'=8,'ba'=4] {'wa_1'}, use_global_device_ids=true, to_apply=%region_1.2 | all-reduce | flops 4096 | bytes 32768 | tf_op jit(solution)/shard_map/psum | solution.py:20
  53.5 34.2 %psum.44 = f32[4,8,128]{2,0,1:T(4,128)S(1)} all-reduce(f32[4,8,128]{2,0,1:T(4,128)S(1)} %psum.43), channel_id=1, replica_groups=mesh['wa_0'=2,'wa_1'=4,'wa_2'=8,'ba'=4] {'wa_2'}, use_global_device_ids=true, to_apply=%region_2.3 | all-reduce | flops 4096 | bytes 32768 | tf_op jit(solution)/shard_map/psum | solution.py:20
  87.7 1.3 convolution_bitcast_fusion.1
  89.0 1.1 divide_multiply_fusion.1
  90.2 0.6 fusion.121
  90.9 0.1 pad_add_fusion.1
  91.0 0.3 pad_add_fusion.8
  91.3 0.1 reshape.153
  91.4 1.6 convolution_convert_fusion.1
  93.0 5.1 %fusion.110 = bf16[2,36,1024]{2,1,0:T(8,128)(2,1)S(1)} fusion(bf16[2,1024,320]{1,2,0:T(8,128)(2,1)} %convolution_convert_fusion.1, f32[2,1024,320]{1,2,0:T(8,128)S(1)} %fusion.190, f32[2,1024,320]{1,2,0:T(8,128)} %fusion.88, f32[320]{0:T(512)S(1)} %copy-done.13, bf16[320,320]{1,0:T(8,128)(2,1)S(1)} %copy-done, bf16[320,36]{0,1:T(8,128)(2,1)S(1)} %copy-done.1), kind=kOutput, calls=%fused_computation.118 | convolution fusion | flops 482418688 | bytes 6930176 | tf_op jit(solution)/shard_map/transpose(jvp(vmap()))/dot_general | solution.py:66
  98.3 0.1 pad_add_fusion.15
  98.5 0.7 multiply_reduce_fusion.1
  99.2 1.3 broadcast_in_dim.9
  100.4 4.8 %all-to-all-start = ((f32[64,1,1]{2,1,0:T(1,128)}), f32[64,1,1]{2,1,0:T(1,128)S(1)}, u32[]{:S(2)}, u32[]{:S(2)}) async-start(f32[64,1,1]{2,1,0:T(1,128)} %broadcast_in_dim.9), calls=%async_computation | async-start | bytes 65536 | tf_op jit(solution)/shard_map/all_to_all | solution.py:26
  105.2 0.6 slice_multiply_fusion.1
  106.5 10.6 %all-to-all-done = f32[64,1,1]{2,1,0:T(1,128)S(1)} async-done(((f32[64,1,1]{2,1,0:T(1,128)}), f32[64,1,1]{2,1,0:T(1,128)S(1)}, u32[]{:S(2)}, u32[]{:S(2)}) %all-to-all-start) | async-done | bytes 288 | tf_op jit(solution)/shard_map/all_to_all | solution.py:26
  117.1 0.7 reduce_sum.46
  118.5 1.3 dynamic_update_slice.12
  119.9 1.3 dynamic_update_slice.13
  121.2 0.7 collective-permute-start.1
  121.9 0.6 slice_add_fusion.2
  122.5 8.3 %collective-permute-done.1 = f32[4,8,128]{2,0,1:T(4,128)S(1)} collective-permute-done((f32[4,8,128]{2,0,1:T(4,128)S(1)}, f32[4,8,128]{2,0,1:T(4,128)S(1)}, u32[]{:S(2)}, u32[]{:S(2)}) %collective-permute-start.1) | collective-permute-done | bytes 16416 | tf_op jit(solution)/shard_map/ppermute | solution.py:35
  133.4 1.2 collective-permute-done.3
  134.6 0.1 fusion.235
  135.0 0.1 convert_bitcast_fusion.1
  135.6 0.5 fusion.187
  136.2 1.1 fusion.86
  137.2 1.5 copy-done.16
  138.7 0.9 fusion.97
  139.8 0.2 fusion.178
  140.0 1.3 convolution_bitcast_fusion
  141.3 8.9 %psum.45 = f32[4,8,128]{2,0,1:T(4,128)S(1)} all-reduce(f32[4,8,128]{2,0,1:T(4,128)S(1)} %select_bitcast_fusion), channel_id=1, replica_groups=mesh['wa_0'=2,'wa_1'=4,'wa_2'=8,'ba'=4] {'wa_0'}, use_global_device_ids=true, to_apply=%region_6.7 | all-reduce | flops 4096 | bytes 32768 | tf_op jit(solution)/shard_map/psum | solution.py:20
  150.2 14.3 %psum.46 = f32[4,8,128]{2,0,1:T(4,128)S(1)} all-reduce(f32[4,8,128]{2,0,1:T(4,128)S(1)} %psum.45), channel_id=1, replica_groups=mesh['wa_0'=2,'wa_1'=4,'wa_2'=8,'ba'=4] {'wa_1'}, use_global_device_ids=true, to_apply=%region_7.8 | all-reduce | flops 4096 | bytes 32768 | tf_op jit(solution)/shard_map/psum | solution.py:20
  164.5 32.8 %psum.47 = f32[4,8,128]{2,0,1:T(4,128)S(1)} all-reduce(f32[4,8,128]{2,0,1:T(4,128)S(1)} %psum.46), channel_id=1, replica_groups=mesh['wa_0'=2,'wa_1'=4,'wa_2'=8,'ba'=4] {'wa_2'}, use_global_device_ids=true, to_apply=%region_8.9 | all-reduce | flops 4096 | bytes 32768 | tf_op jit(solution)/shard_map/psum | solution.py:20
  197.3 1.1 divide_multiply_fusion
  198.5 1.3 fusion.120
  199.9 0.1 pad_add_fusion
  200.0 0.3 pad_add_fusion.2
  200.4 1.6 convolution_convert_fusion
  202.1 5.1 %fusion.115 = bf16[2,36,1024]{2,1,0:T(8,128)(2,1)S(1)} fusion(bf16[2,1024,320]{1,2,0:T(8,128)(2,1)} %convolution_convert_fusion, f32[2,1024,320]{1,2,0:T(8,128)S(1)} %fusion.187, f32[2,1024,320]{1,2,0:T(8,128)} %copy-done.16, f32[320]{0:T(512)S(1)} %copy-done.11, bf16[320,320]{1,0:T(8,128)(2,1)S(1)} %copy-done, bf16[320,36]{0,1:T(8,128)(2,1)S(1)} %copy-done.2), kind=kOutput, calls=%fused_computation.119 | convolution fusion | flops 482418688 | bytes 6930176 | tf_op jit(solution)/shard_map/transpose(jvp(vmap()))/dot_general | solution.py:66
  207.1 0.1 reshape.158
  207.4 0.1 pad_add_fusion.14
  207.5 0.7 multiply_reduce_fusion
  208.2 0.6 broadcast_in_dim.11
  208.8 15.8 %all_to_all.12 = f32[64,1,1]{2,1,0:T(1,128)S(1)} all-to-all(f32[64,1,1]{2,1,0:T(1,128)S(1)} %broadcast_in_dim.11), channel_id=1, replica_groups=mesh['wa_0'=2,'wa_1'=4,'wa_2'=8,'ba'=4] {'wa_0','wa_1','wa_2'}, dimensions={0} | all-to-all | bytes 512 | tf_op jit(solution)/shard_map/all_to_all | solution.py:26
  224.6 0.7 reduce_sum.49
  225.9 1.3 dynamic_update_slice.14
  227.3 1.3 dynamic_update_slice.15
  228.6 0.7 collective-permute-start.4
  229.4 8.8 %collective-permute-done.4 = f32[4,8,128]{2,0,1:T(4,128)S(1)} collective-permute-done((f32[4,8,128]{2,0,1:T(4,128)S(1)}, f32[4,8,128]{2,0,1:T(4,128)S(1)}, u32[]{:S(2)}, u32[]{:S(2)}) %collective-permute-start.4) | collective-permute-done | bytes 16416 | tf_op jit(solution)/shard_map/ppermute | solution.py:35
  238.2 0.6 copy.97
  (92 shorter events, 2.8 us)
Async XLA Ops:
  0.0 24.1 %copy-start = (bf16[320,320]{1,0:T(8,128)(2,1)S(1)}, bf16[320,320]{1,0:T(8,128)(2,1)}, u32[]{:S(2)}) copy-start(bf16[320,320]{1,0:T(8,128)(2,1)} %param.16) | copy-start | bytes 614404
  0.8 21.1 %collective-permute-start = (f32[4,8,128]{2,0,1:T(4,128)S(1)}, f32[4,8,128]{2,0,1:T(4,128)S(1)}, u32[]{:S(2)}, u32[]{:S(2)}) collective-permute-start(f32[4,8,128]{2,0,1:T(4,128)S(1)} %get-tuple-element.43), channel_id=1, source_target_pairs={{0,252},{4,0},{8,4},{12,8},{16,12},{20,16},{24,20},{28,24},{32,28}... | collective-permute-start | bytes 49160 | tf_op jit(solution)/shard_map/ppermute | solution.py:35
  11.4 1.2 copy-start.14
  12.0 110.0 %collective-permute-start.2 = (f32[128]{0:T(128)}, f32[128]{0:T(128)}, u32[]{:S(2)}, u32[]{:S(2)}) collective-permute-start(f32[128]{0:T(128)} %slice.200), channel_id=1, source_target_pairs={{0,4},{4,8},{8,12},{12,16},{16,20},{20,24},{24,28},{28,32},{32,36}... | collective-permute-start | bytes 1544 | tf_op jit(solution)/shard_map/ppermute | solution.py:35
  13.9 12.7 %copy-start.12 = (f32[320]{0:T(512)}, f32[320]{0:T(512)S(1)}, u32[]{:S(2)}) copy-start(f32[320]{0:T(512)S(1)} %get-tuple-element.6) | copy-start | bytes 3844
  24.1 2.6 %copy-start.3 = (bf16[36,320]{1,0:T(8,128)(2,1)S(1)}, bf16[36,320]{1,0:T(8,128)(2,1)}, u32[]{:S(2)}) copy-start(bf16[36,320]{1,0:T(8,128)(2,1)} %param.17) | copy-start | bytes 69124
  29.4 60.8 %copy-start.7 = (f32[64,4]{0,1:T(4,128)S(1)}, f32[64,4]{0,1:T(4,128)}, u32[]{:S(2)}) copy-start(f32[64,4]{0,1:T(4,128)} %param.19) | copy-start | bytes 3076
  90.2 2.9 %copy-start.1 = (bf16[320,36]{0,1:T(8,128)(2,1)S(1)}, bf16[320,36]{0,1:T(8,128)(2,1)}, u32[]{:S(2)}) copy-start(bf16[320,36]{0,1:T(8,128)(2,1)} %param.15) | copy-start | bytes 69124
  90.2 2.8 %copy-start.13 = (f32[320]{0:T(512)S(1)}, f32[320]{0:T(512)}, u32[]{:S(2)}) copy-start(f32[320]{0:T(512)} %copy-done.12) | copy-start | bytes 3844
  93.0 12.2 %copy-start.6 = (f32[2,4,8,128]{3,2,1,0:T(8,128)S(1)}, f32[2,4,8,128]{3,2,1,0:T(8,128)}, u32[]{:S(2)}) copy-start(f32[2,4,8,128]{3,2,1,0:T(8,128)} %param.11) | copy-start | bytes 98308
  93.0 28.9 %copy-start.15 = (f32[256]{0:T(256)S(1)}, f32[256]{0:T(256)}, u32[]{:S(2)}) copy-start(f32[256]{0:T(256)} %copy-done.14) | copy-start | bytes 3076
  98.3 37.9 %copy-start.10 = (f32[320]{0:T(512)S(1)}, f32[320]{0:T(512)}, u32[]{:S(2)}) copy-start(f32[320]{0:T(512)} %get-tuple-element.5) | copy-start | bytes 3844
  100.4 16.6 %all-to-all-start = ((f32[64,1,1]{2,1,0:T(1,128)}), f32[64,1,1]{2,1,0:T(1,128)S(1)}, u32[]{:S(2)}, u32[]{:S(2)}) async-start(f32[64,1,1]{2,1,0:T(1,128)} %broadcast_in_dim.9), calls=%async_computation | async-start | bytes 65536 | tf_op jit(solution)/shard_map/all_to_all | solution.py:26
  121.2 9.5 %collective-permute-start.1 = (f32[4,8,128]{2,0,1:T(4,128)S(1)}, f32[4,8,128]{2,0,1:T(4,128)S(1)}, u32[]{:S(2)}, u32[]{:S(2)}) collective-permute-start(f32[4,8,128]{2,0,1:T(4,128)S(1)} %slice.230), channel_id=1, source_target_pairs={{0,4},{4,8},{8,12},{12,16},{16,20},{20,24},{24,28},{28,32},{32,36}... | collective-permute-start | bytes 49160 | tf_op jit(solution)/shard_map/ppermute | solution.py:35
  122.5 10.9 %copy-start.8 = (f32[128]{0:T(128)}, f32[128]{0:T(128)S(1)}, u32[]{:S(2)}) copy-start(f32[128]{0:T(128)S(1)} %slice_add_fusion.2) | copy-start | bytes 1540
  130.8 3.8 %collective-permute-start.3 = (f32[4,8,128]{2,0,1:T(4,128)S(1)}, f32[4,8,128]{2,0,1:T(4,128)S(1)}, u32[]{:S(2)}, u32[]{:S(2)}) collective-permute-start(f32[4,8,128]{2,0,1:T(4,128)S(1)} %divide_add_fusion.1), channel_id=1, source_target_pairs={{0,252},{4,0},{8,4},{12,8},{16,12},{20,16},{24,20},{28,24},{32,28}... | collective-permute-start | bytes 49160 | tf_op jit(solution)/shard_map/ppermute | solution.py:35
  137.2 1.5 copy-start.16
  198.5 1.9 copy-start.4
  198.5 3.6 %copy-start.2 = (bf16[320,36]{0,1:T(8,128)(2,1)S(1)}, bf16[320,36]{0,1:T(8,128)(2,1)}, u32[]{:S(2)}) copy-start(bf16[320,36]{0,1:T(8,128)(2,1)} %param.15) | copy-start | bytes 69124
  199.8 2.2 copy-start.11
  202.0 36.1 %copy-start.5 = (f32[1,4,8,128]{3,2,1,0:T(8,128)S(1)}, f32[1,4,8,128]{3,2,1,0:T(8,128)}, u32[]{:S(2)}) copy-start(f32[1,4,8,128]{3,2,1,0:T(8,128)} %get-tuple-element.42) | copy-start | bytes 49156
  202.0 36.1 %copy-start.9 = (f32[128]{0:T(128)S(1)}, f32[128]{0:T(128)}, u32[]{:S(2)}) copy-start(f32[128]{0:T(128)} %copy-done.8) | copy-start | bytes 1540
  228.6 9.5 %collective-permute-start.4 = (f32[4,8,128]{2,0,1:T(4,128)S(1)}, f32[4,8,128]{2,0,1:T(4,128)S(1)}, u32[]{:S(2)}, u32[]{:S(2)}) collective-permute-start(f32[4,8,128]{2,0,1:T(4,128)S(1)} %slice.235), channel_id=1, source_target_pairs={{0,4},{4,8},{8,12},{12,16},{16,20},{20,24},{24,28},{28,32},{32,36}... | collective-permute-start | bytes 49160 | tf_op jit(solution)/shard_map/ppermute | solution.py:35
where the time goes:
time: 240 us; the launch traced here: 239 us
  blocking collectives  130 us (54%)
  matrix products  29.2 us (12%)
  waiting for transfers between devices  28.9 us (12%)
  local copies, waits for them, and re-layouts  16.4 us (7%)
  starting transfers between devices  16.1 us (7%)
  between operations  11.6 us (5%)
  other arithmetic  6.67 us (3%)
    psum x6, blocking collectives, broadcast_by_axis(): shard = lax.psum(shard, axis)  114 us
    ppermute x5, waiting for transfers between devices, passed_along(): lax.ppermute(shard, axis, [(i, (i + by) % length) for i in range(length)])  18.3 us
    all_to_all x1, blocking collectives, from_everyone(): return lax.all_to_all(copies, axis, split_axis=0, concat_axis=0, tiled=True)  15.8 us
    dot_general x4, matrix products, denoise(): jnp.dot(w_in, stacked, preferred_element_type=jnp.float32)  12 us
    ppermute x5, starting transfers between devices, passed_along(): lax.ppermute(shard, axis, [(i, (i + by) % length) for i in range(length)])  11.3 us
    all_to_all x1, waiting for transfers between devices, from_everyone(): return lax.all_to_all(copies, axis, split_axis=0, concat_axis=0, tiled=True)  10.6 us
    dot_general x6, matrix products, percept(): jnp.einsum('fc,chw->fhw', w_feat, cleaned, precision=lax.Precision.HIGHEST)  6.83 us
    dot_general x4, matrix products, denoise(): jnp.dot(w_out, joined, preferred_element_type=jnp.float32)  6.8 us
  transfers between devices with their start and end apart: 6, of which 4 were waited for; matrix products, arithmetic and copies ran while one was open for 12% of the time, Pallas kernels for 0%

commit v1 on v0

--- a/solution.py
+++ b/solution.py
@@ -17,7 +17,7 @@
 def broadcast_by_axis(shard, axes, root):
     shard = jnp.where(lax.axis_index(axes) == root, shard, jnp.zeros_like(shard))
     for axis in axes:
-        shard = lax.psum(shard, axis)
+        shard = jnp.sum(lax.all_gather(shard, axis), axis=0)
     return shard
 
 

time: 240 us -> 220 us (0.917)
  blocking collectives: 130 us -> 105 us
  starting transfers between devices: 16.1 us -> 21.3 us
    psum x6 -> x0, blocking collectives: 114 us -> none  [broadcast_by_axis(): shard = lax.psum(shard, axis)]
    all_gather x0 -> x6, blocking collectives: none -> 85 us  [broadcast_by_axis(): shard = jnp.sum(lax.all_gather(shard, axis), axis=0)]
    all_to_all x1, starting transfers between devices: 4.77 us -> 9.81 us  [from_everyone(): return lax.all_to_all(copies, axis, split_axis=0, concat_axis=0, tiled=True)]
    all_to_all x1, blocking collectives: 15.8 us -> 19.7 us  [from_everyone(): return lax.all_to_all(copies, axis, split_axis=0, concat_axis=0, tiled=True)]
    unnamed x49 -> x71, local copies, waits for them, and re-layouts: 3.3 us -> 4.85 us
  transfers between devices with their start and end apart: 6 -> 6, of which waited for: 4 -> 4; matrix products, arithmetic and copies ran while one was open for 12% -> 13% of each run, Pallas kernels for 0% -> 0%
where the time goes in v1:
time: 220 us; the launch traced here: 219 us
  blocking collectives  105 us (48%)
  waiting for transfers between devices  29.1 us (13%)
  matrix products  26.8 us (12%)
  starting transfers between devices  21.3 us (10%)
  local copies, waits for them, and re-layouts  17.9 us (8%)
  between operations  11.5 us (5%)
  other arithmetic  7.99 us (4%)
    all_gather x6, blocking collectives, broadcast_by_axis(): shard = jnp.sum(lax.all_gather(shard, axis), axis=0)  85 us
    all_to_all x1, blocking collectives, from_everyone(): return lax.all_to_all(copies, axis, split_axis=0, concat_axis=0, tiled=True)  19.7 us
    ppermute x5, waiting for transfers between devices, passed_along(): lax.ppermute(shard, axis, [(i, (i + by) % length) for i in range(length)])  18.3 us
    dot_general x4, matrix products, denoise(): jnp.dot(w_in, stacked, preferred_element_type=jnp.float32)  12 us
    ppermute x5, starting transfers between devices, passed_along(): lax.ppermute(shard, axis, [(i, (i + by) % length) for i in range(length)])  11.5 us
    all_to_all x1, waiting for transfers between devices, from_everyone(): return lax.all_to_all(copies, axis, split_axis=0, concat_axis=0, tiled=True)  10.7 us
    all_to_all x1, starting transfers between devices, from_everyone(): return lax.all_to_all(copies, axis, split_axis=0, concat_axis=0, tiled=True)  9.81 us
    dot_general x4, matrix products, denoise(): jnp.dot(w_out, joined, preferred_element_type=jnp.float32)  6.55 us
  transfers between devices with their start and end apart: 6, of which 4 were waited for; matrix products, arithmetic and copies ran while one was open for 13% of the time, Pallas kernels for 0%

profile of v1, /device:TPU:2, one launch (start us, length us, event | category | flops | bytes accessed | tf_op | source)
XLA Modules:
  0.0 219.4 jit_solution(18068420607774785316)
XLA Ops:
  0.0 0.8 fusion.241
  0.8 9.9 %collective-permute-start = (f32[4,8,128]{2,0,1:T(4,128)S(1)}, f32[4,8,128]{2,0,1:T(4,128)S(1)}, u32[]{:S(2)}, u32[]{:S(2)}) collective-permute-start(f32[4,8,128]{2,0,1:T(4,128)S(1)} %get-tuple-element.43), channel_id=1, source_target_pairs={{0,252},{4,0},{8,4},{12,8},{16,12},{20,16},{24,20},{28,24},{32,28}... | collective-permute-start | bytes 49160 | tf_op jit(solution)/shard_map/ppermute | solution.py:35
  10.6 0.7 broadcast_add_fusion
  11.4 0.5 slice.200
  11.9 0.6 fusion.243
  12.5 1.3 slice_reduce_fusion
  13.9 1.3 fusion.242
  22.4 1.3 fusion.190
  23.7 1.0 fusion.88
  24.8 1.5 copy-done.26
  26.3 0.9 fusion.94
  27.4 0.8 fusion.180
  28.2 5.9 %all_gather.32 = f32[2,4,8,128]{3,2,1,0:T(8,128)S(1)} all-gather(f32[1,4,8,128]{3,2,1,0:T(8,128)S(1)} %copy.150), channel_id=1, replica_groups=mesh['wa_0'=2,'wa_1'=4,'wa_2'=8,'ba'=4] {'wa_0'}, dimensions={0}, use_global_device_ids=true | all-gather | bytes 49152 | tf_op jit(solution)/shard_map/all_gather | solution.py:20
  34.1 11.9 %all-gather = f32[16,8,128]{2,1,0:T(8,128)S(1)} all-gather(f32[4,8,128]{2,1,0:T(8,128)S(1)} %reduce_sum.99), channel_id=2, replica_groups=mesh['wa_0'=2,'wa_1'=4,'wa_2'=8,'ba'=4] {'wa_1'}, dimensions={0}, use_global_device_ids=true | all-gather | bytes 81920 | tf_op jit(solution)/shard_map/all_gather | solution.py:20
  45.9 24.9 %all-gather.1 = f32[32,8,128]{2,1,0:T(8,128)S(1)} all-gather(f32[4,8,128]{2,1,0:T(8,128)S(1)} %reduce_sum.100), channel_id=3, replica_groups=mesh['wa_0'=2,'wa_1'=4,'wa_2'=8,'ba'=4] {'wa_2'}, dimensions={0}, use_global_device_ids=true | all-gather | bytes 147456 | tf_op jit(solution)/shard_map/all_gather | solution.py:20
  70.8 1.3 convolution_bitcast_fusion.1
  72.1 1.1 divide_multiply_fusion.1
  73.3 1.3 fusion.121
  74.7 0.1 pad_add_fusion.1
  74.8 0.3 pad_add_fusion.8
  75.2 2.4 %convolution_convert_fusion.1 = bf16[2,1024,320]{1,2,0:T(8,128)(2,1)} fusion(bf16[2,36,1024]{2,1,0:T(8,128)(2,1)S(1)} %reshape.151, bf16[36,320]{1,0:T(8,128)(2,1)} %param.17), kind=kOutput, calls=%fused_computation.101 | convolution fusion | flops 47185920 | bytes 1481216 | tf_op jit(solution)/shard_map/transpose(jvp(vmap()))/dot_general | solution.py:70
  77.6 5.1 %fusion.110 = bf16[2,36,1024]{2,1,0:T(8,128)(2,1)S(1)} fusion(bf16[2,1024,320]{1,2,0:T(8,128)(2,1)} %convolution_convert_fusion.1, f32[2,1024,320]{1,2,0:T(8,128)S(1)} %fusion.190, f32[2,1024,320]{1,2,0:T(8,128)} %copy-done.26, f32[320]{0:T(512)S(1)} %copy-done.23, bf16[320,320]{1,0:T(8,128)(2,1)S(1)} %copy-done, bf16[320,36]{0,1:T(8,128)(2,1)S(1)} %copy-done.11), kind=kOutput, calls=%fused_computation.118 | convolution fusion | flops 482418688 | bytes 6930176 | tf_op jit(solution)/shard_map/transpose(jvp(vmap()))/dot_general | solution.py:66
  82.7 0.1 reshape.152
  82.9 0.1 pad_add_fusion.15
  83.0 0.7 multiply_reduce_fusion.1
  83.8 1.3 broadcast_in_dim.9
  85.0 9.8 %all-to-all-start = ((f32[64,1,1]{2,1,0:T(1,128)}), f32[64,1,1]{2,1,0:T(1,128)S(1)}, u32[]{:S(2)}, u32[]{:S(2)}) async-start(f32[64,1,1]{2,1,0:T(1,128)} %broadcast_in_dim.9), calls=%async_computation | async-start | bytes 65536 | tf_op jit(solution)/shard_map/all_to_all | solution.py:26
  94.9 0.6 slice_multiply_fusion.1
  96.1 10.7 %all-to-all-done = f32[64,1,1]{2,1,0:T(1,128)S(1)} async-done(((f32[64,1,1]{2,1,0:T(1,128)}), f32[64,1,1]{2,1,0:T(1,128)S(1)}, u32[]{:S(2)}, u32[]{:S(2)}) %all-to-all-start) | async-done | bytes 288 | tf_op jit(solution)/shard_map/all_to_all | solution.py:26
  106.9 0.7 reduce_sum.103
  108.3 1.3 dynamic_update_slice.12
  109.8 1.3 dynamic_update_slice.13
  111.1 0.9 collective-permute-start.1
  111.9 0.6 slice_add_fusion.2
  112.5 8.3 %collective-permute-done.1 = f32[4,8,128]{2,0,1:T(4,128)S(1)} collective-permute-done((f32[4,8,128]{2,0,1:T(4,128)S(1)}, f32[4,8,128]{2,0,1:T(4,128)S(1)}, u32[]{:S(2)}, u32[]{:S(2)}) %collective-permute-start.1) | collective-permute-done | bytes 16416 | tf_op jit(solution)/shard_map/ppermute | solution.py:35
  123.4 1.3 collective-permute-done.3
  124.6 0.1 fusion.237
  125.1 0.1 convert_bitcast_fusion.1
  125.6 0.5 fusion.187
  126.2 1.0 fusion.86
  127.3 1.5 copy-done.27
  128.8 0.9 fusion.97
  129.9 0.8 fusion.178
  130.6 0.6 convolution_bitcast_fusion
  131.3 5.9 %all_gather.37 = f32[2,4,8,128]{3,2,1,0:T(8,128)S(1)} all-gather(f32[1,4,8,128]{3,2,1,0:T(8,128)S(1)} %copy.166), channel_id=1, replica_groups=mesh['wa_0'=2,'wa_1'=4,'wa_2'=8,'ba'=4] {'wa_0'}, dimensions={0}, use_global_device_ids=true | all-gather | bytes 49152 | tf_op jit(solution)/shard_map/all_gather | solution.py:20
  137.2 11.9 %all-gather.2 = f32[16,8,128]{2,1,0:T(8,128)S(1)} all-gather(f32[4,8,128]{2,1,0:T(8,128)S(1)} %reduce_sum.105), channel_id=4, replica_groups=mesh['wa_0'=2,'wa_1'=4,'wa_2'=8,'ba'=4] {'wa_1'}, dimensions={0}, use_global_device_ids=true | all-gather | bytes 81920 | tf_op jit(solution)/shard_map/all_gather | solution.py:20
  149.1 24.6 %all-gather.3 = f32[32,8,128]{2,1,0:T(8,128)S(1)} all-gather(f32[4,8,128]{2,1,0:T(8,128)S(1)} %reduce_sum.106), channel_id=5, replica_groups=mesh['wa_0'=2,'wa_1'=4,'wa_2'=8,'ba'=4] {'wa_2'}, dimensions={0}, use_global_device_ids=true | all-gather | bytes 147456 | tf_op jit(solution)/shard_map/all_gather | solution.py:20
  173.7 0.5 divide_multiply_fusion
  174.2 1.3 fusion.120
  175.5 0.1 pad_add_fusion
  175.7 0.3 pad_add_fusion.2
  176.0 0.1 reshape.155
  176.1 2.4 %convolution_convert_fusion = bf16[2,1024,320]{1,2,0:T(8,128)(2,1)} fusion(bf16[2,36,1024]{2,1,0:T(8,128)(2,1)S(1)} %reshape.155, bf16[36,320]{1,0:T(8,128)(2,1)} %param.17), kind=kOutput, calls=%fused_computation.100 | convolution fusion | flops 47185920 | bytes 1481216 | tf_op jit(solution)/shard_map/transpose(jvp(vmap()))/dot_general | solution.py:70
  178.5 5.1 %fusion.115 = bf16[2,36,1024]{2,1,0:T(8,128)(2,1)S(1)} fusion(bf16[2,1024,320]{1,2,0:T(8,128)(2,1)} %convolution_convert_fusion, f32[2,1024,320]{1,2,0:T(8,128)S(1)} %fusion.187, f32[2,1024,320]{1,2,0:T(8,128)} %copy-done.27, f32[320]{0:T(512)S(1)} %copy-done.21, bf16[320,320]{1,0:T(8,128)(2,1)S(1)} %copy-done, bf16[320,36]{0,1:T(8,128)(2,1)S(1)} %copy-done.12), kind=kOutput, calls=%fused_computation.119 | convolution fusion | flops 482418688 | bytes 6930176 | tf_op jit(solution)/shard_map/transpose(jvp(vmap()))/dot_general | solution.py:66
  183.8 0.1 pad_add_fusion.14
  183.9 0.7 multiply_reduce_fusion
  184.6 0.6 broadcast_in_dim.11
  185.3 19.7 %all_to_all.12 = f32[64,1,1]{2,1,0:T(1,128)S(1)} all-to-all(f32[64,1,1]{2,1,0:T(1,128)S(1)} %broadcast_in_dim.11), channel_id=1, replica_groups=mesh['wa_0'=2,'wa_1'=4,'wa_2'=8,'ba'=4] {'wa_0','wa_1','wa_2'}, dimensions={0} | all-to-all | bytes 512 | tf_op jit(solution)/shard_map/all_to_all | solution.py:26
  205.0 0.7 reduce_sum.109
  206.5 1.3 dynamic_update_slice.14
  207.9 1.3 dynamic_update_slice.15
  209.2 0.7 collective-permute-start.4
  209.9 8.8 %collective-permute-done.4 = f32[4,8,128]{2,0,1:T(4,128)S(1)} collective-permute-done((f32[4,8,128]{2,0,1:T(4,128)S(1)}, f32[4,8,128]{2,0,1:T(4,128)S(1)}, u32[]{:S(2)}, u32[]{:S(2)}) %collective-permute-start.4) | collective-permute-done | bytes 16416 | tf_op jit(solution)/shard_map/ppermute | solution.py:35
  218.8 0.6 copy.177
  (122 shorter events, 3.0 us)
Async XLA Ops:
  0.0 23.7 %copy-start = (bf16[320,320]{1,0:T(8,128)(2,1)S(1)}, bf16[320,320]{1,0:T(8,128)(2,1)}, u32[]{:S(2)}) copy-start(bf16[320,320]{1,0:T(8,128)(2,1)} %param.16) | copy-start | bytes 614404
  0.8 20.7 %collective-permute-start = (f32[4,8,128]{2,0,1:T(4,128)S(1)}, f32[4,8,128]{2,0,1:T(4,128)S(1)}, u32[]{:S(2)}, u32[]{:S(2)}) collective-permute-start(f32[4,8,128]{2,0,1:T(4,128)S(1)} %get-tuple-element.43), channel_id=1, source_target_pairs={{0,252},{4,0},{8,4},{12,8},{16,12},{20,16},{24,20},{28,24},{32,28}... | collective-permute-start | bytes 49160 | tf_op jit(solution)/shard_map/ppermute | solution.py:35
  11.4 1.1 copy-start.24
  11.9 100.0 %collective-permute-start.2 = (f32[128]{0:T(128)}, f32[128]{0:T(128)}, u32[]{:S(2)}, u32[]{:S(2)}) collective-permute-start(f32[128]{0:T(128)} %slice.200), channel_id=1, source_target_pairs={{0,4},{4,8},{8,12},{12,16},{16,20},{20,24},{24,28},{28,32},{32,36}... | collective-permute-start | bytes 1544 | tf_op jit(solution)/shard_map/ppermute | solution.py:35
  13.9 10.9 %copy-start.22 = (f32[320]{0:T(512)}, f32[320]{0:T(512)S(1)}, u32[]{:S(2)}) copy-start(f32[320]{0:T(512)S(1)} %get-tuple-element.6) | copy-start | bytes 3844
  21.5 5.8 %copy-start.1 = (f32[1,4,8,128]{3,1,2,0:T(4,128)}, f32[1,4,8,128]{3,1,2,0:T(4,128)S(1)}, u32[]{:S(2)}) copy-start(f32[1,4,8,128]{3,1,2,0:T(4,128)S(1)} %get-tuple-element.39) | copy-start | bytes 49156
  21.5 5.8 %copy-start.3 = (f32[1,4,8,128]{3,1,2,0:T(4,128)}, f32[1,4,8,128]{3,1,2,0:T(4,128)S(1)}, u32[]{:S(2)}) copy-start(f32[1,4,8,128]{3,1,2,0:T(4,128)S(1)} %get-tuple-element.40) | copy-start | bytes 49156
  23.7 2.6 %copy-start.13 = (bf16[36,320]{1,0:T(8,128)(2,1)S(1)}, bf16[36,320]{1,0:T(8,128)(2,1)}, u32[]{:S(2)}) copy-start(bf16[36,320]{1,0:T(8,128)(2,1)} %param.17) | copy-start | bytes 69124
  24.8 1.5 copy-start.26
  74.6 2.9 %copy-start.11 = (bf16[320,36]{0,1:T(8,128)(2,1)S(1)}, bf16[320,36]{0,1:T(8,128)(2,1)}, u32[]{:S(2)}) copy-start(bf16[320,36]{0,1:T(8,128)(2,1)} %param.15) | copy-start | bytes 69124
  74.6 2.9 %copy-start.23 = (f32[320]{0:T(512)S(1)}, f32[320]{0:T(512)}, u32[]{:S(2)}) copy-start(f32[320]{0:T(512)} %copy-done.22) | copy-start | bytes 3844
  77.6 17.3 %copy-start.16 = (f32[2,4,8,128]{3,2,1,0:T(8,128)S(1)}, f32[2,4,8,128]{3,2,1,0:T(8,128)}, u32[]{:S(2)}) copy-start(f32[2,4,8,128]{3,2,1,0:T(8,128)} %param.11) | copy-start | bytes 98308
  77.6 30.7 %copy-start.2 = (f32[1,4,8,128]{3,1,2,0:T(4,128)S(1)}, f32[1,4,8,128]{3,1,2,0:T(4,128)}, u32[]{:S(2)}) copy-start(f32[1,4,8,128]{3,1,2,0:T(4,128)} %copy-done.1) | copy-start | bytes 49156
  77.6 30.7 %copy-start.4 = (f32[1,4,8,128]{3,1,2,0:T(4,128)S(1)}, f32[1,4,8,128]{3,1,2,0:T(4,128)}, u32[]{:S(2)}) copy-start(f32[1,4,8,128]{3,1,2,0:T(4,128)} %copy-done.3) | copy-start | bytes 49156
  77.6 30.7 %copy-start.9 = (f32[2,1,4,8,128]{4,2,3,0,1:T(4,128)S(1)}, f32[2,1,4,8,128]{4,2,3,0,1:T(4,128)}, u32[]{:S(2)}) copy-start(f32[2,1,4,8,128]{4,2,3,0,1:T(4,128)} %get-tuple-element.14) | copy-start | bytes 98308
  77.6 34.4 %copy-start.25 = (f32[256]{0:T(256)S(1)}, f32[256]{0:T(256)}, u32[]{:S(2)}) copy-start(f32[256]{0:T(256)} %copy-done.24) | copy-start | bytes 3076
  82.8 43.3 %copy-start.20 = (f32[320]{0:T(512)S(1)}, f32[320]{0:T(512)}, u32[]{:S(2)}) copy-start(f32[320]{0:T(512)} %get-tuple-element.5) | copy-start | bytes 3844
  85.0 21.8 %all-to-all-start = ((f32[64,1,1]{2,1,0:T(1,128)}), f32[64,1,1]{2,1,0:T(1,128)S(1)}, u32[]{:S(2)}, u32[]{:S(2)}) async-start(f32[64,1,1]{2,1,0:T(1,128)} %broadcast_in_dim.9), calls=%async_computation | async-start | bytes 65536 | tf_op jit(solution)/shard_map/all_to_all | solution.py:26
  111.1 9.7 %collective-permute-start.1 = (f32[4,8,128]{2,0,1:T(4,128)S(1)}, f32[4,8,128]{2,0,1:T(4,128)S(1)}, u32[]{:S(2)}, u32[]{:S(2)}) collective-permute-start(f32[4,8,128]{2,0,1:T(4,128)S(1)} %slice.230), channel_id=1, source_target_pairs={{0,4},{4,8},{8,12},{12,16},{16,20},{20,24},{24,28},{28,32},{32,36}... | collective-permute-start | bytes 49160 | tf_op jit(solution)/shard_map/ppermute | solution.py:35
  112.5 13.6 %copy-start.18 = (f32[128]{0:T(128)}, f32[128]{0:T(128)S(1)}, u32[]{:S(2)}) copy-start(f32[128]{0:T(128)S(1)} %slice_add_fusion.2) | copy-start | bytes 1540
  120.8 3.8 %collective-permute-start.3 = (f32[4,8,128]{2,0,1:T(4,128)S(1)}, f32[4,8,128]{2,0,1:T(4,128)S(1)}, u32[]{:S(2)}, u32[]{:S(2)}) collective-permute-start(f32[4,8,128]{2,0,1:T(4,128)S(1)} %divide_add_fusion.1), channel_id=1, source_target_pairs={{0,252},{4,0},{8,4},{12,8},{16,12},{20,16},{24,20},{28,24},{32,28}... | collective-permute-start | bytes 49160 | tf_op jit(solution)/shard_map/ppermute | solution.py:35
  124.7 5.1 %copy-start.5 = (f32[1,4,8,128]{3,1,2,0:T(4,128)}, f32[1,4,8,128]{3,1,2,0:T(4,128)S(1)}, u32[]{:S(2)}) copy-start(f32[1,4,8,128]{3,1,2,0:T(4,128)S(1)} %get-tuple-element.35) | copy-start | bytes 49156
  124.8 5.1 %copy-start.7 = (f32[1,4,8,128]{3,1,2,0:T(4,128)}, f32[1,4,8,128]{3,1,2,0:T(4,128)S(1)}, u32[]{:S(2)}) copy-start(f32[1,4,8,128]{3,1,2,0:T(4,128)S(1)} %get-tuple-element.36) | copy-start | bytes 49156
  126.2 2.6 %copy-start.14 = (bf16[36,320]{1,0:T(8,128)(2,1)S(1)}, bf16[36,320]{1,0:T(8,128)(2,1)}, u32[]{:S(2)}) copy-start(bf16[36,320]{1,0:T(8,128)(2,1)} %param.17) | copy-start | bytes 69124
  127.3 1.5 copy-start.27
  128.8 1.9 copy-start.17
  175.5 2.9 %copy-start.12 = (bf16[320,36]{0,1:T(8,128)(2,1)S(1)}, bf16[320,36]{0,1:T(8,128)(2,1)}, u32[]{:S(2)}) copy-start(bf16[320,36]{0,1:T(8,128)(2,1)} %param.15) | copy-start | bytes 69124
  175.5 2.9 %copy-start.21 = (f32[320]{0:T(512)S(1)}, f32[320]{0:T(512)}, u32[]{:S(2)}) copy-start(f32[320]{0:T(512)} %get-tuple-element.5) | copy-start | bytes 3844
  178.4 28.0 %copy-start.6 = (f32[1,4,8,128]{3,1,2,0:T(4,128)S(1)}, f32[1,4,8,128]{3,1,2,0:T(4,128)}, u32[]{:S(2)}) copy-start(f32[1,4,8,128]{3,1,2,0:T(4,128)} %copy-done.5) | copy-start | bytes 49156
  178.4 28.0 %copy-start.8 = (f32[1,4,8,128]{3,1,2,0:T(4,128)S(1)}, f32[1,4,8,128]{3,1,2,0:T(4,128)}, u32[]{:S(2)}) copy-start(f32[1,4,8,128]{3,1,2,0:T(4,128)} %copy-done.7) | copy-start | bytes 49156
  178.4 28.0 %copy-start.10 = (f32[2,1,4,8,128]{4,2,3,0,1:T(4,128)S(1)}, f32[2,1,4,8,128]{4,2,3,0,1:T(4,128)}, u32[]{:S(2)}) copy-start(f32[2,1,4,8,128]{4,2,3,0,1:T(4,128)} %get-tuple-element.10) | copy-start | bytes 98308
  178.4 40.3 %copy-start.15 = (f32[1,4,8,128]{3,2,1,0:T(8,128)S(1)}, f32[1,4,8,128]{3,2,1,0:T(8,128)}, u32[]{:S(2)}) copy-start(f32[1,4,8,128]{3,2,1,0:T(8,128)} %get-tuple-element.42) | copy-start | bytes 49156
  178.5 40.3 %copy-start.19 = (f32[128]{0:T(128)S(1)}, f32[128]{0:T(128)}, u32[]{:S(2)}) copy-start(f32[128]{0:T(128)} %copy-done.18) | copy-start | bytes 1540
  209.2 9.5 %collective-permute-start.4 = (f32[4,8,128]{2,0,1:T(4,128)S(1)}, f32[4,8,128]{2,0,1:T(4,128)S(1)}, u32[]{:S(2)}, u32[]{:S(2)}) collective-permute-start(f32[4,8,128]{2,0,1:T(4,128)S(1)} %slice.235), channel_id=1, source_target_pairs={{0,4},{4,8},{8,12},{12,16},{16,20},{20,24},{24,28},{28,32},{32,36}... | collective-permute-start | bytes 49160 | tf_op jit(solution)/shard_map/ppermute | solution.py:35
